TPU v7x, 32 devices: a whole 2x2x4 slice. The times are simulated.
32 devices in a mesh: section: 4 (over y, x), row: 8 (over z, core).
Axes of the slice: x: 2, y: 2, z: 4, core: 2. Of those that a mesh axis runs over, the one named last changes fastest.
Arguments:
- omega: bfloat16 [2048, 8192], P('section', 'row'), may hold values from -0.5 to 0.5
- basis: bfloat16 [8192, 1024], P('row', 'section'), may hold values from -6 to 6
- vectors: bfloat16 [4, 8192], P(None, 'row'), may hold values from -6 to 6
Outputs:
- ortho: float32 [4, 8192], P(None, ('row', 'section'))
- coeffs: float32 [4, 1024], P(None, 'section')
All inputs are finite; a program needn't handle non-finite values.
Results may differ from a plain program's by a relative error of at most 0.0021.
Values may be sent and summed in bfloat16 or wider, within the bound.
A program may use at most 64 MiB of HBM per device.

v0:
```python
import jax
import jax.numpy as jnp
from jax import lax
from jax.sharding import PartitionSpec as P


def from_behind(value, axis, steps):
    count = lax.axis_size(axis)
    initial, last = (max(0, -steps), min(count, count - steps))
    return lax.ppermute(value, axis, [(source, source + steps) for source in range(initial, last)])


def from_root(value, axis, source):
    kept = jnp.where(lax.axis_index(axis) == source, value, 0).astype(value.dtype)
    return lax.psum(kept, axis)


def lower_solve(factor, right):
    return lax.linalg.triangular_solve(factor, right, left_side=True, lower=True, transpose_a=False)


def factor_solve(factor, right):
    half = lower_solve(factor, right)
    return lax.linalg.triangular_solve(factor, half, left_side=True, lower=True, transpose_a=True)


def body(omega, basis, vectors):
    hi = lax.Precision.HIGHEST
    sections = lax.axis_size("section")
    my_section = lax.axis_index("section")
    whole = lax.all_gather(omega, "section", axis=0, tiled=True)
    sketch = lax.psum_scatter(
        jnp.dot(whole, basis, preferred_element_type=jnp.float32),
        "row",
        scatter_dimension=0,
        tiled=True,
    )
    probe_term = lax.dot_general(
        vectors, whole, (((1,), (1,)), ((), ())), preferred_element_type=jnp.float32
    )
    probe = lax.psum_scatter(probe_term, "row", scatter_dimension=1, tiled=True)
    gram = lax.psum(jnp.dot(sketch.T, sketch, precision=hi), "row")
    factor = jnp.linalg.cholesky(gram)

    def project(current):
        inner = jnp.dot(current, sketch, precision=hi)
        inner = lax.psum(inner, "row")
        coef = factor_solve(factor, inner.T).T
        return (coef, current - jnp.dot(coef, sketch.T, precision=hi))

    def advance(step, carry):
        current, kept = carry
        coef, moved = project(current)
        active = my_section == step
        kept = jnp.where(active, coef, kept)
        moved = jnp.where(active, moved, current)
        return (from_behind(moved, "section", 1), kept)

    start_coef = jnp.zeros((vectors.shape[0], basis.shape[1]), jnp.float32)
    probe, kept = lax.fori_loop(0, sections - 1, advance, (probe, start_coef))
    coef, moved = project(probe)
    finished = my_section == sections - 1
    kept = jnp.where(finished, coef, kept)
    final = from_root(moved, "section", sections - 1)
    rounded = kept.astype(jnp.bfloat16)
    own_term = lax.dot_general(
        rounded, basis, (((1,), (1,)), ((), ())), preferred_element_type=jnp.float32
    )
    removed = lax.psum_scatter(own_term, "section", scatter_dimension=1, tiled=True)
    width = removed.shape[1]
    mine = lax.dynamic_slice_in_dim(vectors, my_section * width, width, 1)
    remain = mine.astype(jnp.float32) - removed
    small = lax.psum(jnp.dot(final, final.T, precision=hi), "row")
    lower = jnp.linalg.cholesky(small)
    ortho = lower_solve(lower, remain)
    return (ortho, kept)


def solution(mesh):
    return jax.shard_map(
        body,
        mesh=mesh,
        in_specs=(P("section", "row"), P("row", "section"), P(None, "row")),
        out_specs=(P(None, ("row", "section")), P(None, "section")),
        check_vma=False,
    )
```

profile of v0, /device:TPU:0, one launch (start us, length us, event | category | flops | bytes accessed | tf_op | source)
XLA Modules:
  0.0 442.4 jit_solution(2750653464107480190)
XLA Ops:
  7.2 0.7 all-gather.2.cloned.1.call-update
  8.0 57.2 %all-gather.2.cloned.1.call-done = bf16[2048,1024]{1,0:T(8,128)(2,1)} async-done(((bf16[512,1024]{1,0:T(8,128)(2,1)}), bf16[2048,1024]{1,0:T(8,128)(2,1)}) %all-gather.2.cloned.1.call-update) | async-done | bytes 4194320 | tf_op jit(solution)/shard_map/all_gather | solution.py:31
  65.2 4.8 %fusion.36 = f32[2048,256]{1,0:T(8,128)} fusion(bf16[2048,1024]{1,0:T(8,128)(2,1)} %all-gather.2.cloned.1.call-done, bf16[1024,256]{1,0:T(8,128)(2,1)S(1)} %copy-done), kind=kOutput, calls=%fused_computation.78 | convolution fusion | flops 1073741824 | bytes 6815744 | tf_op jit(solution)/shard_map/dot_general | solution.py:33
  70.0 4.4 convolution_bitcast_fusion
  74.5 31.6 %reduce-scatter.8.cloned.1.call-done = f32[256,256]{1,0:T(8,128)} async-done(((f32[2048,256]{1,0:T(8,128)}), f32[256,256]{1,0:T(8,128)}) %reduce-scatter.8.cloned.1.call-update) | async-done | bytes 262160 | tf_op jit(solution)/shard_map/reduce_scatter | solution.py:32
  106.1 2.4 fusion.37
  108.8 30.9 %reduce-scatter.10.cloned.1.call-done = f32[256,4]{1,0:T(8,128)} async-done(((f32[2048,4]{1,0:T(8,128)}), f32[256,4]{1,0:T(8,128)}) %reduce-scatter.10.cloned.1.call-update) | async-done | bytes 4112
  139.7 1.0 copy.18
  140.7 54.8 %all-reduce.3.cloned.1.call-done = f32[256,256]{0,1:T(8,128)} async-done(((f32[256,256]{0,1:T(8,128)}), f32[256,256]{0,1:T(8,128)}) %all-reduce.3.cloned.1.call-update) | async-done | bytes 262160 | tf_op jit(solution)/shard_map/psum | solution.py:42
  195.5 1.1 copy.11
  196.6 1.0 fusion.11
  197.6 11.7 %cholesky.64 = f32[128,128]{1,0:T(8,128)S(1)} custom-call(f32[128,128]{1,0:T(8,128)S(1)} %cholesky.153), custom_call_target="Cholesky" | custom-call | tf_op jit(solution)/shard_map/jit(cholesky)/cholesky | solution.py:43
  209.4 9.8 %custom-call.23 = f32[1,128,128]{1,2,0:T(8,128)S(1)} custom-call(f32[1,128,128]{2,1,0:T(8,128)S(1)} %get-tuple-element.206), custom_call_target="InvertDiagBlocksLowerTriangular" | custom-call | tf_op jit(solution)/shard_map/jit(cholesky)/cholesky | solution.py:43
  219.4 0.3 convolution_subtract_fusion.3
  219.7 11.7 %cholesky.131 = f32[128,128]{1,0:T(8,128)S(1)} custom-call(f32[128,128]{1,0:T(8,128)S(1)} %convolution_subtract_fusion.3), custom_call_target="Cholesky" | custom-call | tf_op jit(solution)/shard_map/jit(cholesky)/cholesky | solution.py:43
  231.4 0.7 compare_reduce_fusion.1
  233.5 4.2 while.27
  233.7 0.7 fusion.105
  234.4 1.3 bitcast_dynamic-update-slice_fusion.4
  235.7 0.7 fusion.105
  236.4 1.3 bitcast_dynamic-update-slice_fusion.4
  237.8 19.7 %custom-call.31 = f32[2,128,128]{1,2,0:T(8,128)S(1)} custom-call(f32[2,128,128]{2,1,0:T(8,128)S(1)} %get-tuple-element.168), custom_call_target="InvertDiagBlocksLowerTriangular" | custom-call | tf_op jit(solution)/shard_map/triangular_solve/custom-call.4 | solution.py:24
  257.4 133.4 %while.26 = (s32[]{:T(128)}, f32[4,256]{1,0:T(4,128)S(1)}, f32[4,256]{1,0:T(4,128)S(1)}, s32[]{:T(128)}, f32[256,256]{1,0:T(8,128)S(1)}, /*index=5*/f32[256,256]{1,0:T(8,128)S(1)}, s32[]{:T(128)}, s32[]{:T(128)}, s32[]{:T(128)}) while((s32[]{:T(128)}, f32[4,256]{1,0:T(4,128)S(1)}, f32[4,256]{1,0:T(4,128)S(1)}, s32[]{:T(128)}, ...), condition=%wide.region_9.12_spmd.clone, body=%wide.region_7.0_spmd.clone.sunk | while | flops 11149320 | bytes 1659231 | solution.py:60
  257.6 4.1 while.28
  257.6 0.7 fusion.106
  258.3 1.3 bitcast_dynamic-update-slice_fusion.5
  259.6 0.7 fusion.106
  260.3 1.3 bitcast_dynamic-update-slice_fusion.5
  261.6 19.7 %custom-call.37 = f32[2,128,128]{1,2,0:T(8,128)S(1)} custom-call(f32[2,128,128]{2,1,0:T(8,128)S(1)} %get-tuple-element.303), custom_call_target="InvertDiagBlocksLowerTriangular" | custom-call | tf_op jit(solution)/shard_map/while/body/eval_jaxpr/triangular_solve/custom-call.4 | solution.py:24
  281.5 13.7 %psum.45 = f32[256,4]{0,1:T(4,128)S(1)} all-reduce(f32[256,4]{0,1:T(4,128)S(1)} %fusion.99), channel_id=1, replica_groups=mesh['section'=4,'row'=8] {'row'}, use_global_device_ids=true, to_apply=%region_8.8 | all-reduce | flops 1024 | bytes 8192 | tf_op jit(solution)/shard_map/while/body/eval_jaxpr/psum | solution.py:47
  296.4 0.3 fusion.104
  296.7 3.4 collective-permute-start
  300.1 1.3 collective-permute-done
  301.5 4.1 while.28
  301.5 0.7 fusion.106
  302.2 1.3 bitcast_dynamic-update-slice_fusion.5
  303.6 0.7 fusion.106
  304.2 1.3 bitcast_dynamic-update-slice_fusion.5
  305.6 19.7 %custom-call.37 = f32[2,128,128]{1,2,0:T(8,128)S(1)} custom-call(f32[2,128,128]{2,1,0:T(8,128)S(1)} %get-tuple-element.303), custom_call_target="InvertDiagBlocksLowerTriangular" | custom-call | tf_op jit(solution)/shard_map/while/body/eval_jaxpr/triangular_solve/custom-call.4 | solution.py:24
  325.5 13.6 %psum.45 = f32[256,4]{0,1:T(4,128)S(1)} all-reduce(f32[256,4]{0,1:T(4,128)S(1)} %fusion.99), channel_id=1, replica_groups=mesh['section'=4,'row'=8] {'row'}, use_global_device_ids=true, to_apply=%region_8.8 | all-reduce | flops 1024 | bytes 8192 | tf_op jit(solution)/shard_map/while/body/eval_jaxpr/psum | solution.py:47
  340.2 0.3 fusion.104
  340.6 4.2 collective-permute-start
  344.8 1.3 collective-permute-done
  346.2 4.1 while.28
  346.2 0.7 fusion.106
  346.9 1.3 bitcast_dynamic-update-slice_fusion.5
  348.2 0.7 fusion.106
  348.9 1.3 bitcast_dynamic-update-slice_fusion.5
  350.3 19.7 %custom-call.37 = f32[2,128,128]{1,2,0:T(8,128)S(1)} custom-call(f32[2,128,128]{2,1,0:T(8,128)S(1)} %get-tuple-element.303), custom_call_target="InvertDiagBlocksLowerTriangular" | custom-call | tf_op jit(solution)/shard_map/while/body/eval_jaxpr/triangular_solve/custom-call.4 | solution.py:24
  370.2 13.6 %psum.45 = f32[256,4]{0,1:T(4,128)S(1)} all-reduce(f32[256,4]{0,1:T(4,128)S(1)} %fusion.99), channel_id=1, replica_groups=mesh['section'=4,'row'=8] {'row'}, use_global_device_ids=true, to_apply=%region_8.8 | all-reduce | flops 1024 | bytes 8192 | tf_op jit(solution)/shard_map/while/body/eval_jaxpr/psum | solution.py:47
  384.9 0.3 fusion.104
  385.2 4.3 collective-permute-start
  389.6 1.3 collective-permute-done
  391.1 13.6 %psum.40 = f32[256,4]{0,1:T(4,128)S(1)} all-reduce(f32[256,4]{0,1:T(4,128)S(1)} %fusion.38), channel_id=1, replica_groups=mesh['section'=4,'row'=8] {'row'}, use_global_device_ids=true, to_apply=%region_10.13 | all-reduce | flops 1024 | bytes 8192 | tf_op jit(solution)/shard_map/psum | solution.py:47
  405.9 1.0 convolution_bitcast_fusion.1
  407.0 0.3 fusion.10
  407.2 11.0 %psum.41 = f32[4,256]{1,0:T(4,128)S(1)} all-reduce(f32[4,256]{1,0:T(4,128)S(1)} %fusion.10), channel_id=1, replica_groups=mesh['section'=4,'row'=8] {'section'}, use_global_device_ids=true, to_apply=%region_11.14 | all-reduce | flops 1024 | bytes 8192 | tf_op jit(solution)/shard_map/psum | solution.py:15
  418.3 13.6 %psum.42 = f32[4,4]{0,1:T(4,128)S(1)} all-reduce(f32[4,4]{0,1:T(4,128)S(1)} %fusion.39), channel_id=1, replica_groups=mesh['section'=4,'row'=8] {'row'}, use_global_device_ids=true, to_apply=%region_12.15 | all-reduce | flops 16 | bytes 128 | tf_op jit(solution)/shard_map/psum | solution.py:73
  432.0 0.4 cholesky.144
  432.4 0.6 compare_reduce_fusion
  433.1 0.6 fusion.25
  433.7 0.3 custom-call.24
  434.1 1.0 copy.20
  435.0 0.8 fusion.22
  (84 shorter events, 6.9 us)
Async XLA Ops:
  7.2 58.0 %copy-start = (bf16[1024,256]{1,0:T(8,128)(2,1)S(1)}, bf16[1024,256]{1,0:T(8,128)(2,1)}, u32[]{:S(2)}) copy-start(bf16[1024,256]{1,0:T(8,128)(2,1)} %param.10) | copy-start | bytes 1572868
  7.2 58.0 %all-gather.2.cloned.1.call-start = ((), (), s32[]{:S(2)}) async-start(), calls=%async_computation.3 | async-start | bytes 5242880 | tf_op jit(solution)/shard_map/all_gather | solution.py:31
  7.9 62.1 %copy-start.3 = (bf16[4,1024]{1,0:T(4,128)(2,1)S(1)}, bf16[4,1024]{1,0:T(4,128)(2,1)}, u32[]{:S(2)}) copy-start(bf16[4,1024]{1,0:T(4,128)(2,1)} %param.11) | copy-start | bytes 24580
  7.9 98.2 %reduce-scatter.8.cloned.1.call-start = ((), (), s32[]{:S(2)}) async-start(), calls=%async_computation.4 | async-start | bytes 2359296 | tf_op jit(solution)/shard_map/reduce_scatter | solution.py:32
  70.0 69.7 %reduce-scatter.10.cloned.1.call-start = ((), (), s32[]{:S(2)}) async-start(), calls=%async_computation.6 | async-start | bytes 1179648
  74.5 121.0 %all-reduce.3.cloned.1.call-start = ((), (), s32[]{:S(2)}) async-start(), calls=%async_computation.5 | async-start | bytes 524288 | tf_op jit(solution)/shard_map/psum | solution.py:42
  106.1 151.3 %copy-start.1 = (f32[256,256]{1,0:T(8,128)S(1)}, f32[256,256]{1,0:T(8,128)}, u32[]{:S(2)}) copy-start(f32[256,256]{1,0:T(8,128)} %reduce-scatter.8.cloned.1.call-done) | copy-start | bytes 786436
  108.5 325.5 %reduce-scatter.12.cloned.1.call-start = ((), (), s32[]{:S(2)}) async-start(), calls=%async_computation.7 | async-start | bytes 655360
  296.7 4.7 %collective-permute-start = (f32[4,256]{1,0:T(4,128)S(1)}, f32[4,256]{1,0:T(4,128)S(1)}, u32[]{:S(2)}, u32[]{:S(2)}) collective-permute-start(f32[4,256]{1,0:T(4,128)S(1)} %fusion.104), channel_id=1, source_target_pairs={{0,8},{8,16},{16,24},{1,9},{9,17},{17,25},{2,10},{10,18},{18,26},{... | collective-permute-start | bytes 12296 | tf_op jit(solution)/shard_map/while/body/eval_jaxpr/ppermute | solution.py:10
  340.6 5.6 %collective-permute-start = (f32[4,256]{1,0:T(4,128)S(1)}, f32[4,256]{1,0:T(4,128)S(1)}, u32[]{:S(2)}, u32[]{:S(2)}) collective-permute-start(f32[4,256]{1,0:T(4,128)S(1)} %fusion.104), channel_id=1, source_target_pairs={{0,8},{8,16},{16,24},{1,9},{9,17},{17,25},{2,10},{10,18},{18,26},{... | collective-permute-start | bytes 12296 | tf_op jit(solution)/shard_map/while/body/eval_jaxpr/ppermute | solution.py:10
  385.2 5.6 %collective-permute-start = (f32[4,256]{1,0:T(4,128)S(1)}, f32[4,256]{1,0:T(4,128)S(1)}, u32[]{:S(2)}, u32[]{:S(2)}) collective-permute-start(f32[4,256]{1,0:T(4,128)S(1)} %fusion.104), channel_id=1, source_target_pairs={{0,8},{8,16},{16,24},{1,9},{9,17},{17,25},{2,10},{10,18},{18,26},{... | collective-permute-start | bytes 12296 | tf_op jit(solution)/shard_map/while/body/eval_jaxpr/ppermute | solution.py:10
  405.9 30.0 %copy-start.2 = (f32[4,256]{1,0:T(4,128)}, f32[4,256]{1,0:T(4,128)S(1)}, u32[]{:S(2)}) copy-start(f32[4,256]{1,0:T(4,128)S(1)} %bitcast_select_fusion.1) | copy-start | bytes 12292
Sparse Core Ops, SparseCore 0:
  9.8 55.2 all-gather.1
  70.1 35.9 reduce-scatter.7
  108.4 31.2 reduce-scatter.9
  141.9 53.5 all-reduce.2
  407.1 25.7 reduce-scatter.11
where the time goes:
time: 443 us; the launch traced here: 442 us
  waiting for transfers between devices  179 us (40%)
  other arithmetic  116 us (26%)
  blocking collectives  79.1 us (18%)
  matrix products  20.6 us (5%)
  local copies, waits for them, and re-layouts  19.6 us (4%)
  between operations  15.2 us (3%)
  starting transfers between devices  12.4 us (3%)
    another operation x16, other arithmetic, factor_solve(): lax.linalg.triangular_solve(factor, half, left_side=True, lower=True, tra...  78.8 us
    all_gather x1, waiting for transfers between devices, body(): whole = lax.all_gather(omega, 'section', axis=0, tiled=True)  57.2 us
    psum x1, waiting for transfers between devices, body(): gram = lax.psum(jnp.dot(sketch.T, sketch, precision=hi), 'row')  54.8 us
    psum x4, blocking collectives, project(): inner = lax.psum(inner, 'row')  54.5 us
    another operation x6, other arithmetic, body(): factor = jnp.linalg.cholesky(gram)  34 us
    unnamed x7, waiting for transfers between devices  31.7 us
    reduce_scatter x1, waiting for transfers between devices, body(): lax.psum_scatter(jnp.dot(whole, basis, preferred_element_type=jnp.float32...  31.6 us
    another operation x28, local copies, waits for them, and re-layouts, factor_solve(): lax.linalg.triangular_solve(factor, half, left_side=True, lower=True, tra...  16.4 us
  transfers between devices with their start and end apart: 8, of which 7 were waited for; matrix products, arithmetic and copies ran while one was open for 2% of the time, Pallas kernels for 0%

commit v1 on v0

--- a/solution.py
+++ b/solution.py
@@ -44,7 +44,9 @@
 
     def project(current):
         inner = jnp.dot(current, sketch, precision=hi)
-        inner = lax.psum(inner, "row")
+        inner = inner
+        for hop in (1, 2, 4):
+            inner = inner + lax.ppermute(inner, "row", [(dev, dev ^ hop) for dev in range(8)])
         coef = factor_solve(factor, inner.T).T
         return (coef, current - jnp.dot(coef, sketch.T, precision=hi))
 

time: 443 us -> 412 us (0.930)
  blocking collectives: 79.1 us -> 24.6 us
  waiting for transfers between devices: 179 us -> 196 us
  starting transfers between devices: 12.4 us -> 20.3 us
    psum x4 -> x0, blocking collectives: 54.5 us -> none  [project(): inner = lax.psum(inner, 'row')]
    ppermute x0 -> x12, waiting for transfers between devices: none -> 17 us  [project(): lax.ppermute(inner, 'row', [(dev, dev ^ hop) for dev in range(8)])]
    ppermute x0 -> x12, starting transfers between devices: none -> 7.95 us  [project(): lax.ppermute(inner, 'row', [(dev, dev ^ hop) for dev in range(8)])]
  transfers between devices with their start and end apart: 8 -> 20, of which waited for: 7 -> 15; matrix products, arithmetic and copies ran while one was open for 2% -> 25% of each run, Pallas kernels for 0% -> 0%
where the time goes in v1:
time: 412 us
  waiting for transfers between devices  196 us (48%)
  other arithmetic  116 us (28%)
  blocking collectives  24.6 us (6%)
  matrix products  20.5 us (5%)
  starting transfers between devices  20.3 us (5%)
  local copies, waits for them, and re-layouts  18.5 us (4%)
  between operations  15.2 us (4%)
    another operation x16, other arithmetic, factor_solve(): lax.linalg.triangular_solve(factor, half, left_side=True, lower=True, tra...  78.9 us
    all_gather x1, waiting for transfers between devices, body(): whole = lax.all_gather(omega, 'section', axis=0, tiled=True)  57.2 us
    psum x1, waiting for transfers between devices, body(): gram = lax.psum(jnp.dot(sketch.T, sketch, precision=hi), 'row')  54.8 us
    another operation x6, other arithmetic, body(): factor = jnp.linalg.cholesky(gram)  34 us
    unnamed x7, waiting for transfers between devices  31.7 us
    reduce_scatter x1, waiting for transfers between devices, body(): lax.psum_scatter(jnp.dot(whole, basis, preferred_element_type=jnp.float32...  31.6 us
    ppermute x12, waiting for transfers between devices, project(): lax.ppermute(inner, 'row', [(dev, dev ^ hop) for dev in range(8)])  17 us
    another operation x28, local copies, waits for them, and re-layouts, factor_solve(): lax.linalg.triangular_solve(factor, half, left_side=True, lower=True, tra...  15.3 us
  transfers between devices with their start and end apart: 20, of which 15 were waited for; matrix products, arithmetic and copies ran while one was open for 25% of the time, Pallas kernels for 0%

profile of v1, /device:TPU:0, one launch (start us, length us, event | category | flops | bytes accessed | tf_op | source)
XLA Modules:
  0.0 411.8 jit_solution(8188052149994774571)
XLA Ops:
  7.2 0.7 all-gather.2.cloned.1.call-update
  8.0 57.2 %all-gather.2.cloned.1.call-done = bf16[2048,1024]{1,0:T(8,128)(2,1)} async-done(((bf16[512,1024]{1,0:T(8,128)(2,1)}), bf16[2048,1024]{1,0:T(8,128)(2,1)}) %all-gather.2.cloned.1.call-update) | async-done | bytes 4194320 | tf_op jit(solution)/shard_map/all_gather | solution.py:31
  65.2 4.8 %fusion.38 = f32[2048,256]{1,0:T(8,128)} fusion(bf16[2048,1024]{1,0:T(8,128)(2,1)} %all-gather.2.cloned.1.call-done, bf16[1024,256]{1,0:T(8,128)(2,1)S(1)} %copy-done), kind=kOutput, calls=%fused_computation.82 | convolution fusion | flops 1073741824 | bytes 6815744 | tf_op jit(solution)/shard_map/dot_general | solution.py:33
  70.0 4.4 %convolution_bitcast_fusion = f32[2048,4]{1,0:T(8,128)} fusion(bf16[4,1024]{1,0:T(4,128)(2,1)S(1)} %copy-done.3, bf16[2048,1024]{1,0:T(8,128)(2,1)} %all-gather.2.cloned.1.call-done), kind=kOutput, calls=%fused_computation.25 | convolution fusion | flops 16777216 | bytes 4235264
  74.5 31.6 %reduce-scatter.8.cloned.1.call-done = f32[256,256]{1,0:T(8,128)} async-done(((f32[2048,256]{1,0:T(8,128)}), f32[256,256]{1,0:T(8,128)}) %reduce-scatter.8.cloned.1.call-update) | async-done | bytes 262160 | tf_op jit(solution)/shard_map/reduce_scatter | solution.py:32
  106.1 2.4 fusion.39
  108.8 30.9 %reduce-scatter.10.cloned.1.call-done = f32[256,4]{1,0:T(8,128)} async-done(((f32[2048,4]{1,0:T(8,128)}), f32[256,4]{1,0:T(8,128)}) %reduce-scatter.10.cloned.1.call-update) | async-done | bytes 4112
  139.7 1.0 copy.18
  140.7 54.8 %all-reduce.3.cloned.1.call-done = f32[256,256]{0,1:T(8,128)} async-done(((f32[256,256]{0,1:T(8,128)}), f32[256,256]{0,1:T(8,128)}) %all-reduce.3.cloned.1.call-update) | async-done | bytes 262160 | tf_op jit(solution)/shard_map/psum | solution.py:42
  195.5 1.1 copy.11
  196.6 1.0 fusion.12
  197.6 11.7 %cholesky.64 = f32[128,128]{1,0:T(8,128)S(1)} custom-call(f32[128,128]{1,0:T(8,128)S(1)} %cholesky.153), custom_call_target="Cholesky" | custom-call | tf_op jit(solution)/shard_map/jit(cholesky)/cholesky | solution.py:43
  209.4 9.8 %custom-call.23 = f32[1,128,128]{1,2,0:T(8,128)S(1)} custom-call(f32[1,128,128]{2,1,0:T(8,128)S(1)} %get-tuple-element.206), custom_call_target="InvertDiagBlocksLowerTriangular" | custom-call | tf_op jit(solution)/shard_map/jit(cholesky)/cholesky | solution.py:43
  219.7 11.7 %cholesky.131 = f32[128,128]{1,0:T(8,128)S(1)} custom-call(f32[128,128]{1,0:T(8,128)S(1)} %convolution_subtract_fusion.2), custom_call_target="Cholesky" | custom-call | tf_op jit(solution)/shard_map/jit(cholesky)/cholesky | solution.py:43
  231.4 0.7 compare_reduce_fusion.1
  233.3 110.6 %while.26 = (s32[]{:T(128)}, f32[4,256]{1,0:T(4,128)S(1)}, f32[4,256]{1,0:T(4,128)S(1)}, s32[]{:T(128)}, f32[256,256]{1,0:T(8,128)S(1)}, /*index=5*/f32[256,256]{1,0:T(8,128)S(1)}, s32[]{:T(128)}, s32[]{:T(128)}, s32[]{:T(128)}) while((s32[]{:T(128)}, f32[4,256]{1,0:T(4,128)S(1)}, f32[4,256]{1,0:T(4,128)S(1)}, s32[]{:T(128)}, ...), condition=%wide.region_8.11_spmd.clone, body=%wide.region_7.10_spmd.clone.sunk | while | flops 11151368 | bytes 1737183 | solution.py:62
  233.8 1.1 collective-permute-done
  235.5 3.1 collective-permute-done.1
  238.6 1.5 collective-permute-start.2
  240.1 3.8 while.28
  240.1 0.6 fusion.106
  240.7 1.3 bitcast_dynamic-update-slice_fusion.5
  242.0 0.6 fusion.106
  242.6 1.3 bitcast_dynamic-update-slice_fusion.5
  243.9 19.7 %custom-call.37 = f32[2,128,128]{1,2,0:T(8,128)S(1)} custom-call(f32[2,128,128]{2,1,0:T(8,128)S(1)} %get-tuple-element.303), custom_call_target="InvertDiagBlocksLowerTriangular" | custom-call | tf_op jit(solution)/shard_map/while/body/eval_jaxpr/triangular_solve/custom-call.4 | solution.py:24
  265.1 3.4 collective-permute-start.3
  268.5 1.3 collective-permute-done.3
  270.1 1.1 collective-permute-done
  271.7 3.1 collective-permute-done.1
  274.8 1.5 collective-permute-start.2
  276.3 3.8 while.28
  276.4 0.6 fusion.106
  276.9 1.3 bitcast_dynamic-update-slice_fusion.5
  278.3 0.6 fusion.106
  278.8 1.3 bitcast_dynamic-update-slice_fusion.5
  280.1 19.7 %custom-call.37 = f32[2,128,128]{1,2,0:T(8,128)S(1)} custom-call(f32[2,128,128]{2,1,0:T(8,128)S(1)} %get-tuple-element.303), custom_call_target="InvertDiagBlocksLowerTriangular" | custom-call | tf_op jit(solution)/shard_map/while/body/eval_jaxpr/triangular_solve/custom-call.4 | solution.py:24
  301.3 4.2 %collective-permute-start.3 = (f32[4,256]{1,0:T(4,128)S(1)}, f32[4,256]{1,0:T(4,128)S(1)}, u32[]{:S(2)}, u32[]{:S(2)}) collective-permute-start(f32[4,256]{1,0:T(4,128)S(1)} %fusion.104), channel_id=1, source_target_pairs={{0,8},{8,16},{16,24},{1,9},{9,17},{17,25},{2,10},{10,18},{18,26},{... | collective-permute-start | bytes 12296 | tf_op jit(solution)/shard_map/while/body/eval_jaxpr/ppermute | solution.py:10
  305.6 1.3 collective-permute-done.3
  307.1 1.1 collective-permute-done
  308.8 3.1 collective-permute-done.1
  311.9 1.5 collective-permute-start.2
  313.4 3.8 while.28
  313.4 0.6 fusion.106
  314.0 1.3 bitcast_dynamic-update-slice_fusion.5
  315.9 1.3 bitcast_dynamic-update-slice_fusion.5
  317.2 19.7 %custom-call.37 = f32[2,128,128]{1,2,0:T(8,128)S(1)} custom-call(f32[2,128,128]{2,1,0:T(8,128)S(1)} %get-tuple-element.303), custom_call_target="InvertDiagBlocksLowerTriangular" | custom-call | tf_op jit(solution)/shard_map/while/body/eval_jaxpr/triangular_solve/custom-call.4 | solution.py:24
  338.3 4.3 %collective-permute-start.3 = (f32[4,256]{1,0:T(4,128)S(1)}, f32[4,256]{1,0:T(4,128)S(1)}, u32[]{:S(2)}, u32[]{:S(2)}) collective-permute-start(f32[4,256]{1,0:T(4,128)S(1)} %fusion.104), channel_id=1, source_target_pairs={{0,8},{8,16},{16,24},{1,9},{9,17},{17,25},{2,10},{10,18},{18,26},{... | collective-permute-start | bytes 12296 | tf_op jit(solution)/shard_map/while/body/eval_jaxpr/ppermute | solution.py:10
  342.7 1.3 collective-permute-done.3
  344.2 1.2 collective-permute-done.4
  345.9 3.1 collective-permute-done.5
  349.0 1.5 collective-permute-start.6
  350.5 3.8 while.27
  350.5 0.6 fusion.105
  351.1 1.3 bitcast_dynamic-update-slice_fusion.4
  352.4 0.6 fusion.105
  353.0 1.3 bitcast_dynamic-update-slice_fusion.4
  354.3 19.7 %custom-call.31 = f32[2,128,128]{1,2,0:T(8,128)S(1)} custom-call(f32[2,128,128]{2,1,0:T(8,128)S(1)} %get-tuple-element.168), custom_call_target="InvertDiagBlocksLowerTriangular" | custom-call | tf_op jit(solution)/shard_map/triangular_solve/custom-call.4 | solution.py:24
  375.2 1.1 convolution_bitcast_fusion.1
  376.6 11.1 %psum.22 = f32[4,256]{1,0:T(4,128)S(1)} all-reduce(f32[4,256]{1,0:T(4,128)S(1)} %fusion.11), channel_id=1, replica_groups=mesh['section'=4,'row'=8] {'section'}, use_global_device_ids=true, to_apply=%region_9.12 | all-reduce | flops 1024 | bytes 8192 | tf_op jit(solution)/shard_map/psum | solution.py:15
  387.8 13.6 %psum.23 = f32[4,4]{0,1:T(4,128)S(1)} all-reduce(f32[4,4]{0,1:T(4,128)S(1)} %fusion.41), channel_id=1, replica_groups=mesh['section'=4,'row'=8] {'row'}, use_global_device_ids=true, to_apply=%region_10.13 | all-reduce | flops 16 | bytes 128 | tf_op jit(solution)/shard_map/psum | solution.py:75
  401.9 0.6 compare_reduce_fusion
  402.5 0.7 fusion.27
  403.5 1.0 copy.20
  404.5 0.8 fusion.24
  (116 shorter events, 11.8 us)
Async XLA Ops:
  7.2 58.0 %copy-start = (bf16[1024,256]{1,0:T(8,128)(2,1)S(1)}, bf16[1024,256]{1,0:T(8,128)(2,1)}, u32[]{:S(2)}) copy-start(bf16[1024,256]{1,0:T(8,128)(2,1)} %param.10) | copy-start | bytes 1572868
  7.2 58.0 %all-gather.2.cloned.1.call-start = ((), (), s32[]{:S(2)}) async-start(), calls=%async_computation.3 | async-start | bytes 5242880 | tf_op jit(solution)/shard_map/all_gather | solution.py:31
  7.9 62.1 %copy-start.3 = (bf16[4,1024]{1,0:T(4,128)(2,1)S(1)}, bf16[4,1024]{1,0:T(4,128)(2,1)}, u32[]{:S(2)}) copy-start(bf16[4,1024]{1,0:T(4,128)(2,1)} %param.11) | copy-start | bytes 24580
  7.9 98.2 %reduce-scatter.8.cloned.1.call-start = ((), (), s32[]{:S(2)}) async-start(), calls=%async_computation.4 | async-start | bytes 2359296 | tf_op jit(solution)/shard_map/reduce_scatter | solution.py:32
  70.0 69.7 %reduce-scatter.10.cloned.1.call-start = ((), (), s32[]{:S(2)}) async-start(), calls=%async_computation.6 | async-start | bytes 1179648
  74.5 121.1 %all-reduce.3.cloned.1.call-start = ((), (), s32[]{:S(2)}) async-start(), calls=%async_computation.5 | async-start | bytes 524288 | tf_op jit(solution)/shard_map/psum | solution.py:42
  106.1 127.2 %copy-start.1 = (f32[256,256]{1,0:T(8,128)S(1)}, f32[256,256]{1,0:T(8,128)}, u32[]{:S(2)}) copy-start(f32[256,256]{1,0:T(8,128)} %reduce-scatter.8.cloned.1.call-done) | copy-start | bytes 786436
  108.5 295.0 %reduce-scatter.12.cloned.1.call-start = ((), (), s32[]{:S(2)}) async-start(), calls=%async_computation.7 | async-start | bytes 655360
  233.8 1.2 collective-permute-start
  235.0 3.6 collective-permute-start.1
  238.6 25.0 %collective-permute-start.2 = (f32[4,256]{1,0:T(4,128)S(1)}, f32[4,256]{1,0:T(4,128)S(1)}, u32[]{:S(2)}, u32[]{:S(2)}) collective-permute-start(f32[4,256]{1,0:T(4,128)S(1)} %add.125), channel_id=1, source_target_pairs={{0,4},{1,5},{2,6},{3,7},{4,0},{5,1},{6,2},{7,3},{8,12},{9,13},{10,... | collective-permute-start | bytes 12296 | tf_op jit(solution)/shard_map/while/body/eval_jaxpr/ppermute | solution.py:49
  265.1 4.7 %collective-permute-start.3 = (f32[4,256]{1,0:T(4,128)S(1)}, f32[4,256]{1,0:T(4,128)S(1)}, u32[]{:S(2)}, u32[]{:S(2)}) collective-permute-start(f32[4,256]{1,0:T(4,128)S(1)} %fusion.104), channel_id=1, source_target_pairs={{0,8},{8,16},{16,24},{1,9},{9,17},{17,25},{2,10},{10,18},{18,26},{... | collective-permute-start | bytes 12296 | tf_op jit(solution)/shard_map/while/body/eval_jaxpr/ppermute | solution.py:10
  270.0 1.2 collective-permute-start
  271.2 3.6 collective-permute-start.1
  274.8 25.0 %collective-permute-start.2 = (f32[4,256]{1,0:T(4,128)S(1)}, f32[4,256]{1,0:T(4,128)S(1)}, u32[]{:S(2)}, u32[]{:S(2)}) collective-permute-start(f32[4,256]{1,0:T(4,128)S(1)} %add.125), channel_id=1, source_target_pairs={{0,4},{1,5},{2,6},{3,7},{4,0},{5,1},{6,2},{7,3},{8,12},{9,13},{10,... | collective-permute-start | bytes 12296 | tf_op jit(solution)/shard_map/while/body/eval_jaxpr/ppermute | solution.py:49
  301.3 5.6 %collective-permute-start.3 = (f32[4,256]{1,0:T(4,128)S(1)}, f32[4,256]{1,0:T(4,128)S(1)}, u32[]{:S(2)}, u32[]{:S(2)}) collective-permute-start(f32[4,256]{1,0:T(4,128)S(1)} %fusion.104), channel_id=1, source_target_pairs={{0,8},{8,16},{16,24},{1,9},{9,17},{17,25},{2,10},{10,18},{18,26},{... | collective-permute-start | bytes 12296 | tf_op jit(solution)/shard_map/while/body/eval_jaxpr/ppermute | solution.py:10
  307.0 1.2 collective-permute-start
  308.2 3.6 collective-permute-start.1
  311.9 25.0 %collective-permute-start.2 = (f32[4,256]{1,0:T(4,128)S(1)}, f32[4,256]{1,0:T(4,128)S(1)}, u32[]{:S(2)}, u32[]{:S(2)}) collective-permute-start(f32[4,256]{1,0:T(4,128)S(1)} %add.125), channel_id=1, source_target_pairs={{0,4},{1,5},{2,6},{3,7},{4,0},{5,1},{6,2},{7,3},{8,12},{9,13},{10,... | collective-permute-start | bytes 12296 | tf_op jit(solution)/shard_map/while/body/eval_jaxpr/ppermute | solution.py:49
  338.3 5.6 %collective-permute-start.3 = (f32[4,256]{1,0:T(4,128)S(1)}, f32[4,256]{1,0:T(4,128)S(1)}, u32[]{:S(2)}, u32[]{:S(2)}) collective-permute-start(f32[4,256]{1,0:T(4,128)S(1)} %fusion.104), channel_id=1, source_target_pairs={{0,8},{8,16},{16,24},{1,9},{9,17},{17,25},{2,10},{10,18},{18,26},{... | collective-permute-start | bytes 12296 | tf_op jit(solution)/shard_map/while/body/eval_jaxpr/ppermute | solution.py:10
  344.2 1.2 collective-permute-start.4
  345.4 3.6 collective-permute-start.5
  349.0 25.0 %collective-permute-start.6 = (f32[4,256]{1,0:T(4,128)S(1)}, f32[4,256]{1,0:T(4,128)S(1)}, u32[]{:S(2)}, u32[]{:S(2)}) collective-permute-start(f32[4,256]{1,0:T(4,128)S(1)} %add.96), channel_id=1, source_target_pairs={{0,4},{1,5},{2,6},{3,7},{4,0},{5,1},{6,2},{7,3},{8,12},{9,13},{10,... | collective-permute-start | bytes 12296 | tf_op jit(solution)/shard_map/ppermute | solution.py:49
  375.2 30.1 %copy-start.2 = (f32[4,256]{1,0:T(4,128)}, f32[4,256]{1,0:T(4,128)S(1)}, u32[]{:S(2)}) copy-start(f32[4,256]{1,0:T(4,128)S(1)} %bitcast_select_fusion.1) | copy-start | bytes 12292
Sparse Core Ops, SparseCore 0:
  9.8 55.2 all-gather.1
  70.1 35.9 reduce-scatter.7
  108.4 31.2 reduce-scatter.9
  141.9 53.5 all-reduce.2
  376.4 26.6 reduce-scatter.11
